TPU v7x, 512 devices: a whole 4x8x8 slice. The times are simulated.
512 devices in a mesh: sub: 16 (over x, z_lo), blk: 32 (over z_hi, y, core).
Axes of the slice: x: 4, y: 8, z: 8 (z_hi: 2, z_lo: 4; z = z_hi * 4 + z_lo), core: 2. Of those that a mesh axis runs over, the one named last changes fastest.
Arguments:
- schur: bfloat16 [16, 8192, 8192], P('sub', 'blk'), as said below
- inverse_blocks: float32 [16, 64, 128, 128], P('sub', 'blk'), as said below
- loads: float32 [16, 32, 8192], P('sub', None, 'blk'), may hold values from -6 to 6
- share_list: int32 [16, 16, 4], P('sub'), may hold values from -1 to 63, as said below
- multiplicity: int32 [16, 64], P('sub', 'blk'), may hold values from 1 to 2, as said below
Outputs:
- solution: float32 [16, 32, 8192], P('sub', None, 'blk')
- misfit: float32 [32, 96], replicated
Inputs may be any that keep to these rules, and one draw needn't show every extreme that they name: share_list[i, j, s] is the local block of subdomain i that holds the s-th block it shares with subdomain j, or -1 for an empty slot; share_list[j, i, s] is the same block in the numbering of j; the used slots of a pair come first and are as many both ways; share_list[i, i, :] is -1; no block of a subdomain appears twice in its list; at most 4 blocks a pair. multiplicity[i, k] is 2 where block k of subdomain i appears in share_list[i], else 1. `schur`: each local Schur complement is a full dense matrix. `inverse_blocks`: full dense blocks.
All inputs are finite; a program needn't handle non-finite values.
Results may differ from a plain program's by a relative error of at most 0.0026.
Values may be sent and summed in bfloat16 or wider, within the bound.
A program may use at most 64 MiB of HBM per device.

v0:
```python
import functools

import jax
import jax.numpy as jnp
from jax import lax
from jax.sharding import Mesh
from jax.sharding import PartitionSpec as P

ITERS = 2
SUB = ("sub_0", "sub_1")
BLK = ("blk_0", "blk_1", "blk_2")
SUB_BLK = ("sub_0", "sub_1", "blk_0", "blk_1", "blk_2")


FULL_PRECISION = lax.Precision.HIGHEST


def copy_for_each(value, axis):
    copies = jnp.broadcast_to(value, (lax.axis_size(axis), *value.shape))
    return lax.all_to_all(copies, axis, split_axis=0, concat_axis=0, tiled=True)


def joined_along(tiles, dim):
    lengths = list(tiles.shape[1:])
    lengths[dim] *= tiles.shape[0]
    return jnp.moveaxis(tiles, 0, dim).reshape(lengths)


def gathered_copies(value, axis, dim):
    tiles = copy_for_each(value, axis)
    return joined_along(tiles, dim)


def over_axes(value, axes):
    return functools.reduce(lax.psum, axes, value)


def body(schur, inverse_blocks, loads, share_list, multiplicity):
    matrix = schur[0]
    inverse = inverse_blocks[0]
    local_rows = matrix.shape[0]
    order_size = matrix.shape[1]
    block_size = inverse.shape[-1]
    block_count = order_size // block_size
    owned_blocks = inverse.shape[0]
    vectors = loads.shape[1]
    subdomains = lax.axis_size(SUB)
    weighting = 1.0 / (order_size * subdomains)
    block_weight = 1.0 / multiplicity[0].astype(jnp.float32)
    row_weight = jnp.repeat(block_weight, block_size)
    slot_blocks = share_list[0].reshape(-1)
    selector = (slot_blocks[:, None] == jnp.arange(block_count, dtype=jnp.int32)[None, :]).astype(
        jnp.float32
    )

    def share(columns):
        count = columns.shape[0]
        blocks = columns.reshape(count, block_count, block_size)
        outgoing = jnp.einsum("mn,knd->mkd", selector, blocks, precision=FULL_PRECISION)
        outgoing = outgoing.reshape(subdomains, -1, count, block_size)
        incoming = lax.all_to_all(outgoing, SUB, split_axis=0, concat_axis=0, tiled=True).reshape(
            -1, count, block_size
        )
        summed = blocks + jnp.einsum("mn,mkd->knd", selector, incoming, precision=FULL_PRECISION)
        return summed.reshape(count, order_size)

    def to_cases(values):
        return share(lax.all_to_all(values, BLK, split_axis=0, concat_axis=1, tiled=True))

    def to_dofs(values):
        return lax.all_to_all(values, BLK, split_axis=1, concat_axis=0, tiled=True)

    def precondition(basis_rows):
        blocks = basis_rows.reshape(vectors, owned_blocks, block_size)
        local = jnp.einsum("kde,pke->pkd", inverse, blocks, precision=FULL_PRECISION)
        local = local * block_weight[None, :, None]
        return to_cases(local.reshape(vectors, local_rows))

    def products(left, right):
        local = lax.dot_general(
            left * row_weight, right, (((1,), (1,)), ((), ())), precision=FULL_PRECISION
        )
        return local * weighting

    def lower_solve(lower, values):
        return jax.scipy.linalg.solve_triangular(lower, values, lower=True)

    right_side = to_dofs(to_cases(loads[0]))
    start_gram = over_axes(products(right_side, right_side), SUB_BLK)
    first = jnp.linalg.cholesky(start_gram)
    basis = [lower_solve(first, right_side)]
    hessen = jnp.zeros((ITERS * vectors, (ITERS + 1) * vectors), jnp.float32)
    for level in range(ITERS):
        rounded = precondition(basis[level]).astype(jnp.bfloat16)
        product = lax.dot_general(
            gathered_copies(rounded, BLK, 0),
            matrix,
            (((1,), (1,)), ((), ())),
            preferred_element_type=jnp.float32,
        )
        image = to_dofs(to_cases(product))
        stacked = jnp.stack(basis)
        local_coef = (
            jnp.einsum("pr,lqr->lpq", image * row_weight, stacked, precision=FULL_PRECISION)
            * weighting
        )
        coefs, whole_gram = (
            over_axes(local_coef, SUB_BLK),
            over_axes(products(image, image), SUB_BLK),
        )
        image = image - jnp.einsum("lpq,lqr->pr", coefs, stacked, precision=FULL_PRECISION)
        gram = whole_gram - jnp.einsum("lpq,lrq->pr", coefs, coefs, precision=FULL_PRECISION)
        lower = jnp.linalg.cholesky(gram)
        basis.append(lower_solve(lower, image))
        row_slice = slice(level * vectors, (level + 1) * vectors)
        for earlier in range(level + 1):
            hessen = hessen.at[row_slice, earlier * vectors : (earlier + 1) * vectors].set(
                coefs[earlier]
            )
        hessen = hessen.at[row_slice, (level + 1) * vectors : (level + 2) * vectors].set(lower)
    target = jnp.zeros((vectors, (ITERS + 1) * vectors), jnp.float32).at[:, :vectors].set(first)
    normal_matrix = jnp.dot(hessen, hessen.T, precision=FULL_PRECISION)
    right_part = jnp.dot(target, hessen.T, precision=FULL_PRECISION)
    factor = jnp.linalg.cholesky(normal_matrix)
    middle = jax.scipy.linalg.solve_triangular(factor, right_part.T, lower=True)
    coeff_t = jax.scipy.linalg.solve_triangular(factor, middle, lower=True, trans=1)
    combine = coeff_t.T
    misfit = target - jnp.dot(combine, hessen, precision=FULL_PRECISION)
    update = jnp.zeros((vectors, local_rows), jnp.float32)
    for level in range(ITERS):
        update = update + jnp.dot(
            combine[:, level * vectors : (level + 1) * vectors],
            basis[level],
            precision=FULL_PRECISION,
        )
    solution = to_dofs(precondition(update))
    return (solution[None], misfit)


def solution(mesh):
    torus = Mesh(mesh.devices.reshape(4, 4, 2, 8, 2), ("sub_0", "sub_1", "blk_0", "blk_1", "blk_2"))
    placed = (
        P(SUB, BLK, None),
        P(SUB, BLK, None, None),
        P(SUB, None, BLK),
        P(SUB, None, None),
        P(SUB, BLK),
    )
    return jax.shard_map(
        body, mesh=torus, in_specs=placed, out_specs=(P(SUB, None, BLK), P()), check_vma=False
    )
```

profile of v0, /device:TPU:1, one launch (start us, length us, event | category | flops | bytes accessed | tf_op | source)
XLA Modules:
  0.0 603.3 jit_solution(12090557508924703576)
XLA Ops:
  1.5 28.8 %all_to_all.179 = f32[32,1,256]{2,1,0:T(1,128)S(1)} all-to-all(f32[32,1,256]{2,1,0:T(1,128)S(1)} %all_to_all.130), channel_id=1, replica_groups=mesh['sub_0'=4,'sub_1'=4,'blk_0'=2,'blk_1'=8,'blk_2'=2] {'blk_0','blk_1'..., dimensions={0} | all-to-all | bytes 65536 | tf_op jit(solution)/shard_map/all_to_all | solution.py:68
  31.8 6.9 %all-to-all-start.1 = ((f32[16,4,1,128]{3,1,2,0:T(4,128)}), f32[16,4,1,128]{3,1,2,0:T(4,128)S(1)}, u32[]{:S(2)}, u32[]{:S(2)}) async-start(f32[16,4,1,128]{3,1,2,0:T(4,128)} %copy.46), calls=%async_computation.1 | async-start | bytes 65536 | tf_op jit(solution)/shard_map/all_to_all | solution.py:61
  40.2 5.3 all-to-all-done.1
  46.4 5.8 all-to-all-start.2
  53.1 11.2 %all-to-all-done.2 = f32[1,32,256]{2,0,1:T(1,128)S(1)} async-done(((f32[1,32,256]{2,0,1:T(1,128)}), f32[1,32,256]{2,0,1:T(1,128)S(1)}, u32[]{:S(2)}, u32[]{:S(2)}) %all-to-all-start.2) | async-done | bytes 32800 | tf_op jit(solution)/shard_map/all_to_all | solution.py:71
  64.4 11.9 %psum.175 = f32[32,32]{0,1:T(8,128)S(1)} all-reduce(f32[32,32]{0,1:T(8,128)S(1)} %convolution_multiply_fusion.7), channel_id=1, replica_groups=mesh['sub_0'=4,'sub_1'=4,'blk_0'=2,'blk_1'=8,'blk_2'=2] {'sub_0'}, use_global_device_ids=true, to_apply=%region_0.0 | all-reduce | flops 1024 | bytes 8192 | tf_op jit(solution)/shard_map/psum | solution.py:35
  76.3 12.3 %psum.176 = f32[32,32]{0,1:T(8,128)S(1)} all-reduce(f32[32,32]{0,1:T(8,128)S(1)} %psum.175), channel_id=1, replica_groups=mesh['sub_0'=4,'sub_1'=4,'blk_0'=2,'blk_1'=8,'blk_2'=2] {'sub_1'}, use_global_device_ids=true, to_apply=%region_1.0 | all-reduce | flops 1024 | bytes 8192 | tf_op jit(solution)/shard_map/psum | solution.py:35
  88.6 9.1 %psum.177 = f32[32,32]{0,1:T(8,128)S(1)} all-reduce(f32[32,32]{0,1:T(8,128)S(1)} %psum.176), channel_id=1, replica_groups=mesh['sub_0'=4,'sub_1'=4,'blk_0'=2,'blk_1'=8,'blk_2'=2] {'blk_0'}, use_global_device_ids=true, to_apply=%region_2.0 | all-reduce | flops 1024 | bytes 8192 | tf_op jit(solution)/shard_map/psum | solution.py:35
  97.7 20.6 %psum.178 = f32[32,32]{0,1:T(8,128)S(1)} all-reduce(f32[32,32]{0,1:T(8,128)S(1)} %psum.177), channel_id=1, replica_groups=mesh['sub_0'=4,'sub_1'=4,'blk_0'=2,'blk_1'=8,'blk_2'=2] {'blk_1'}, use_global_device_ids=true, to_apply=%region_3.0 | all-reduce | flops 1024 | bytes 8192 | tf_op jit(solution)/shard_map/psum | solution.py:35
  118.3 20.1 %psum.179 = f32[32,32]{0,1:T(8,128)S(1)} all-reduce(f32[32,32]{0,1:T(8,128)S(1)} %psum.178), channel_id=1, replica_groups=mesh['sub_0'=4,'sub_1'=4,'blk_0'=2,'blk_1'=8,'blk_2'=2] {'blk_2'}, use_global_device_ids=true, to_apply=%region_4.0 | all-reduce | flops 1024 | bytes 8192 | tf_op jit(solution)/shard_map/psum | solution.py:35
  146.5 20.7 %all_to_all.180 = f32[32,1,256]{2,1,0:T(1,128)S(1)} all-to-all(f32[32,1,256]{2,1,0:T(1,128)S(1)} %bitcast.289), channel_id=1, replica_groups=mesh['sub_0'=4,'sub_1'=4,'blk_0'=2,'blk_1'=8,'blk_2'=2] {'blk_0','blk_1'..., dimensions={0} | all-to-all | bytes 65536 | tf_op jit(solution)/shard_map/all_to_all | solution.py:68
  168.1 9.4 %all_to_all.181 = f32[16,4,1,128]{3,1,2,0:T(4,128)S(1)} all-to-all(f32[16,4,1,128]{3,1,2,0:T(4,128)S(1)} %copy.54), channel_id=1, replica_groups=mesh['sub_0'=4,'sub_1'=4,'blk_0'=2,'blk_1'=8,'blk_2'=2] {'sub_0','sub_1'}, dimensions={0} | all-to-all | bytes 65536 | tf_op jit(solution)/shard_map/all_to_all | solution.py:61
  179.3 3.8 reduce.34
  183.5 25.3 %all_to_all.182 = bf16[32,2,4096]{2,1,0:T(2,128)(2,1)S(1)} all-to-all(bf16[32,2,4096]{2,1,0:T(2,128)(2,1)S(1)} %reshape.632), channel_id=1, replica_groups=mesh['sub_0'=4,'sub_1'=4,'blk_0'=2,'blk_1'=8,'blk_2'=2] {'blk_0','blk_1'..., dimensions={0} | all-to-all | bytes 1048576 | tf_op jit(solution)/shard_map/all_to_all | solution.py:20
  209.3 3.4 fusion.4
  213.4 5.6 all-to-all-start.6
  219.7 11.3 %all-to-all-done.6 = f32[32,1,256]{2,1,0:T(1,128)S(1)} async-done(((f32[32,1,256]{2,1,0:T(1,128)}), f32[32,1,256]{2,1,0:T(1,128)S(1)}, u32[]{:S(2)}, u32[]{:S(2)}) %all-to-all-start.6) | async-done | bytes 32800 | tf_op jit(solution)/shard_map/all_to_all | solution.py:68
  231.8 3.5 all-to-all-start.7
  235.3 6.8 %all-to-all-done.7 = f32[16,4,1,128]{3,1,2,0:T(4,128)S(1)} async-done(((f32[16,4,1,128]{3,1,2,0:T(4,128)}), f32[16,4,1,128]{3,1,2,0:T(4,128)S(1)}, u32[]{:S(2)}, u32[]{:S(2)}) %all-to-all-start.7) | async-done | bytes 32800 | tf_op jit(solution)/shard_map/all_to_all | solution.py:61
  243.0 5.7 all-to-all-start.8
  249.4 11.3 %all-to-all-done.8 = f32[1,32,256]{2,0,1:T(1,128)S(1)} async-done(((f32[1,32,256]{2,0,1:T(1,128)}), f32[1,32,256]{2,0,1:T(1,128)S(1)}, u32[]{:S(2)}, u32[]{:S(2)}) %all-to-all-start.8) | async-done | bytes 32800 | tf_op jit(solution)/shard_map/all_to_all | solution.py:71
  261.0 12.0 %all-reduce.7 = (f32[1,32,32]{2,1,0:T(8,128)S(1)}, f32[32,32]{0,1:T(8,128)S(1)}) all-reduce(f32[1,32,32]{2,1,0:T(8,128)S(1)} %fusion.25, f32[32,32]{0,1:T(8,128)S(1)} %convolution_multiply_fusion.5), channel_id=1, replica_groups=mesh['sub_0'=4,'sub_1'=4,'blk_0'=2,'blk_1'=8,'blk_2'=2] {'sub_0'}, use_global_device_ids=true, to_apply=%region_7.0 | all-reduce | flops 2048 | bytes 16384 | tf_op jit(solution)/shard_map/psum | solution.py:35
  273.1 12.6 %all-reduce.5 = (f32[1,32,32]{2,1,0:T(8,128)S(1)}, f32[32,32]{0,1:T(8,128)S(1)}) all-reduce(f32[1,32,32]{2,1,0:T(8,128)S(1)} %get-tuple-element.88, f32[32,32]{0,1:T(8,128)S(1)} %get-tuple-element.89), channel_id=1, replica_groups=mesh['sub_0'=4,'sub_1'=4,'blk_0'=2,'blk_1'=8,'blk_2'=2] {'sub_1'}, use_global_device_ids=true, to_apply=%region_8.0 | all-reduce | flops 2048 | bytes 16384 | tf_op jit(solution)/shard_map/psum | solution.py:35
  285.7 9.3 %all-reduce.11 = (f32[1,32,32]{2,1,0:T(8,128)S(1)}, f32[32,32]{0,1:T(8,128)S(1)}) all-reduce(f32[1,32,32]{2,1,0:T(8,128)S(1)} %get-tuple-element.84, f32[32,32]{0,1:T(8,128)S(1)} %get-tuple-element.85), channel_id=1, replica_groups=mesh['sub_0'=4,'sub_1'=4,'blk_0'=2,'blk_1'=8,'blk_2'=2] {'blk_0'}, use_global_device_ids=true, to_apply=%region_9.0 | all-reduce | flops 2048 | bytes 16384 | tf_op jit(solution)/shard_map/psum | solution.py:35
  295.0 20.6 %all-reduce.3 = (f32[1,32,32]{2,1,0:T(8,128)S(1)}, f32[32,32]{0,1:T(8,128)S(1)}) all-reduce(f32[1,32,32]{2,1,0:T(8,128)S(1)} %get-tuple-element.96, f32[32,32]{0,1:T(8,128)S(1)} %get-tuple-element.97), channel_id=1, replica_groups=mesh['sub_0'=4,'sub_1'=4,'blk_0'=2,'blk_1'=8,'blk_2'=2] {'blk_1'}, use_global_device_ids=true, to_apply=%region_10.0 | all-reduce | flops 2048 | bytes 16384 | tf_op jit(solution)/shard_map/psum | solution.py:35
  315.6 20.2 %all-reduce.9 = (f32[32,32]{1,0:T(8,128)S(1)}, f32[32,32]{0,1:T(8,128)S(1)}) all-reduce(f32[32,32]{1,0:T(8,128)S(1)} %bitcast.304, f32[32,32]{0,1:T(8,128)S(1)} %get-tuple-element.81), channel_id=1, replica_groups=mesh['sub_0'=4,'sub_1'=4,'blk_0'=2,'blk_1'=8,'blk_2'=2] {'blk_2'}, use_global_device_ids=true, to_apply=%region_11.0 | all-reduce | flops 2048 | bytes 16384 | tf_op jit(solution)/shard_map/psum | solution.py:35
  336.0 2.9 cholesky.105
  345.4 20.7 %all_to_all.183 = f32[32,1,256]{2,1,0:T(1,128)S(1)} all-to-all(f32[32,1,256]{2,1,0:T(1,128)S(1)} %bitcast.290), channel_id=1, replica_groups=mesh['sub_0'=4,'sub_1'=4,'blk_0'=2,'blk_1'=8,'blk_2'=2] {'blk_0','blk_1'..., dimensions={0} | all-to-all | bytes 65536 | tf_op jit(solution)/shard_map/all_to_all | solution.py:68
  366.4 9.9 %all_to_all.184 = f32[16,4,1,128]{3,1,2,0:T(4,128)S(1)} all-to-all(f32[16,4,1,128]{3,1,2,0:T(4,128)S(1)} %copy.65), channel_id=1, replica_groups=mesh['sub_0'=4,'sub_1'=4,'blk_0'=2,'blk_1'=8,'blk_2'=2] {'sub_0','sub_1'}, dimensions={0} | all-to-all | bytes 65536 | tf_op jit(solution)/shard_map/all_to_all | solution.py:61
  377.5 3.8 reduce.35
  381.7 25.6 %all_to_all.185 = bf16[32,2,4096]{2,1,0:T(2,128)(2,1)S(1)} all-to-all(bf16[32,2,4096]{2,1,0:T(2,128)(2,1)S(1)} %reshape.634), channel_id=1, replica_groups=mesh['sub_0'=4,'sub_1'=4,'blk_0'=2,'blk_1'=8,'blk_2'=2] {'blk_0','blk_1'..., dimensions={0} | all-to-all | bytes 1048576 | tf_op jit(solution)/shard_map/all_to_all | solution.py:20
  407.9 3.4 fusion.7
  411.3 16.6 %all_to_all.186 = f32[32,1,256]{2,1,0:T(1,128)S(1)} all-to-all(f32[32,1,256]{2,1,0:T(1,128)S(1)} %copy.66), channel_id=1, replica_groups=mesh['sub_0'=4,'sub_1'=4,'blk_0'=2,'blk_1'=8,'blk_2'=2] {'blk_0','blk_1'..., dimensions={0} | all-to-all | bytes 65536 | tf_op jit(solution)/shard_map/all_to_all | solution.py:68
  428.2 9.4 %all_to_all.187 = f32[16,4,1,128]{3,1,2,0:T(4,128)S(1)} all-to-all(f32[16,4,1,128]{3,1,2,0:T(4,128)S(1)} %copy.67), channel_id=1, replica_groups=mesh['sub_0'=4,'sub_1'=4,'blk_0'=2,'blk_1'=8,'blk_2'=2] {'sub_0','sub_1'}, dimensions={0} | all-to-all | bytes 65536 | tf_op jit(solution)/shard_map/all_to_all | solution.py:61
  438.5 5.6 all-to-all-start.14
  446.3 9.8 %all-to-all-done.14 = f32[1,32,256]{2,0,1:T(1,128)S(1)} async-done(((f32[1,32,256]{2,0,1:T(1,128)}), f32[1,32,256]{2,0,1:T(1,128)S(1)}, u32[]{:S(2)}, u32[]{:S(2)}) %all-to-all-start.14) | async-done | bytes 32800 | tf_op jit(solution)/shard_map/all_to_all | solution.py:71
  456.5 12.4 %all-reduce.6 = (f32[2,32,32]{2,1,0:T(8,128)S(1)}, f32[32,32]{0,1:T(8,128)S(1)}) all-reduce(f32[2,32,32]{2,1,0:T(8,128)S(1)} %fusion.13, f32[32,32]{0,1:T(8,128)S(1)} %convolution_multiply_fusion.4), channel_id=1, replica_groups=mesh['sub_0'=4,'sub_1'=4,'blk_0'=2,'blk_1'=8,'blk_2'=2] {'sub_0'}, use_global_device_ids=true, to_apply=%region_18.0 | all-reduce | flops 3072 | bytes 24576 | tf_op jit(solution)/shard_map/psum | solution.py:35
  468.9 13.3 %all-reduce.4 = (f32[2,32,32]{2,1,0:T(8,128)S(1)}, f32[32,32]{0,1:T(8,128)S(1)}) all-reduce(f32[2,32,32]{2,1,0:T(8,128)S(1)} %get-tuple-element.86, f32[32,32]{0,1:T(8,128)S(1)} %get-tuple-element.87), channel_id=1, replica_groups=mesh['sub_0'=4,'sub_1'=4,'blk_0'=2,'blk_1'=8,'blk_2'=2] {'sub_1'}, use_global_device_ids=true, to_apply=%region_19.0 | all-reduce | flops 3072 | bytes 24576 | tf_op jit(solution)/shard_map/psum | solution.py:35
  482.2 9.6 %all-reduce.10 = (f32[2,32,32]{2,1,0:T(8,128)S(1)}, f32[32,32]{0,1:T(8,128)S(1)}) all-reduce(f32[2,32,32]{2,1,0:T(8,128)S(1)} %get-tuple-element.82, f32[32,32]{0,1:T(8,128)S(1)} %get-tuple-element.83), channel_id=1, replica_groups=mesh['sub_0'=4,'sub_1'=4,'blk_0'=2,'blk_1'=8,'blk_2'=2] {'blk_0'}, use_global_device_ids=true, to_apply=%region_20.0 | all-reduce | flops 3072 | bytes 24576 | tf_op jit(solution)/shard_map/psum | solution.py:35
  491.8 21.3 %all-reduce.2 = (f32[2,32,32]{2,1,0:T(8,128)S(1)}, f32[32,32]{0,1:T(8,128)S(1)}) all-reduce(f32[2,32,32]{2,1,0:T(8,128)S(1)} %get-tuple-element.94, f32[32,32]{0,1:T(8,128)S(1)} %get-tuple-element.95), channel_id=1, replica_groups=mesh['sub_0'=4,'sub_1'=4,'blk_0'=2,'blk_1'=8,'blk_2'=2] {'blk_1'}, use_global_device_ids=true, to_apply=%region_21.0 | all-reduce | flops 3072 | bytes 24576 | tf_op jit(solution)/shard_map/psum | solution.py:35
  513.1 19.9 %all-reduce.8 = (f32[2,32,32]{2,1,0:T(8,128)S(1)}, f32[32,32]{0,1:T(8,128)S(1)}) all-reduce(f32[2,32,32]{2,1,0:T(8,128)S(1)} %get-tuple-element.78, f32[32,32]{0,1:T(8,128)S(1)} %get-tuple-element.79), channel_id=1, replica_groups=mesh['sub_0'=4,'sub_1'=4,'blk_0'=2,'blk_1'=8,'blk_2'=2] {'blk_2'}, use_global_device_ids=true, to_apply=%region_22.0 | all-reduce | flops 3072 | bytes 24576 | tf_op jit(solution)/shard_map/psum | solution.py:35
  533.2 2.9 cholesky.116
  540.2 5.8 cholesky.41
  547.3 4.9 custom-call.15
  553.3 20.7 %all_to_all.188 = f32[32,1,256]{2,1,0:T(1,128)S(1)} all-to-all(f32[32,1,256]{2,1,0:T(1,128)S(1)} %bitcast.291), channel_id=1, replica_groups=mesh['sub_0'=4,'sub_1'=4,'blk_0'=2,'blk_1'=8,'blk_2'=2] {'blk_0','blk_1'..., dimensions={0} | all-to-all | bytes 65536 | tf_op jit(solution)/shard_map/all_to_all | solution.py:68
  574.3 9.7 %all_to_all.189 = f32[16,4,1,128]{3,1,2,0:T(4,128)S(1)} all-to-all(f32[16,4,1,128]{3,1,2,0:T(4,128)S(1)} %copy.77), channel_id=1, replica_groups=mesh['sub_0'=4,'sub_1'=4,'blk_0'=2,'blk_1'=8,'blk_2'=2] {'sub_0','sub_1'}, dimensions={0} | all-to-all | bytes 65536 | tf_op jit(solution)/shard_map/all_to_all | solution.py:61
  584.9 5.8 all-to-all-start.17
  591.5 11.2 %all-to-all-done.17 = f32[1,32,256]{2,0,1:T(1,128)S(1)} async-done(((f32[1,32,256]{2,0,1:T(1,128)}), f32[1,32,256]{2,0,1:T(1,128)S(1)}, u32[]{:S(2)}, u32[]{:S(2)}) %all-to-all-start.17) | async-done | bytes 32800 | tf_op jit(solution)/shard_map/all_to_all | solution.py:71
  (98 shorter events, 43.3 us)
Async XLA Ops:
  0.6 145.5 %copy-start = (f32[1,2,128,128]{3,2,1,0:T(8,128)S(1)}, f32[1,2,128,128]{3,2,1,0:T(8,128)}, u32[]{:S(2)}) copy-start(f32[1,2,128,128]{3,2,1,0:T(8,128)} %param.21) | copy-start | bytes 393220
  31.8 13.7 %all-to-all-start.1 = ((f32[16,4,1,128]{3,1,2,0:T(4,128)}), f32[16,4,1,128]{3,1,2,0:T(4,128)S(1)}, u32[]{:S(2)}, u32[]{:S(2)}) async-start(f32[16,4,1,128]{3,1,2,0:T(4,128)} %copy.46), calls=%async_computation.1 | async-start | bytes 65536 | tf_op jit(solution)/shard_map/all_to_all | solution.py:61
  46.4 17.8 %all-to-all-start.2 = ((f32[1,32,256]{2,0,1:T(1,128)}), f32[1,32,256]{2,0,1:T(1,128)S(1)}, u32[]{:S(2)}, u32[]{:S(2)}) async-start(f32[1,32,256]{2,0,1:T(1,128)} %bitcast.9), calls=%async_computation.2 | async-start | bytes 65536 | tf_op jit(solution)/shard_map/all_to_all | solution.py:71
  183.1 35.9 %copy-start.2 = (s32[2]{0:T(128)S(1)}, s32[2]{0:T(128)}, u32[]{:S(2)}) copy-start(s32[2]{0:T(128)} %constant.236.clone.1) | copy-start | bytes 28
  183.1 47.8 %copy-start.1 = (s32[1,16,4]{1,2,0:T(4,128)S(1)}, s32[1,16,4]{1,2,0:T(4,128)}, u32[]{:S(2)}) copy-start(s32[1,16,4]{1,2,0:T(4,128)} %param.23) | copy-start | bytes 772
  213.4 17.5 %all-to-all-start.6 = ((f32[32,1,256]{2,1,0:T(1,128)}), f32[32,1,256]{2,1,0:T(1,128)S(1)}, u32[]{:S(2)}, u32[]{:S(2)}) async-start(f32[32,1,256]{2,1,0:T(1,128)} %copy.55), calls=%async_computation.6 | async-start | bytes 65536 | tf_op jit(solution)/shard_map/all_to_all | solution.py:68
  231.8 10.3 %all-to-all-start.7 = ((f32[16,4,1,128]{3,1,2,0:T(4,128)}), f32[16,4,1,128]{3,1,2,0:T(4,128)S(1)}, u32[]{:S(2)}, u32[]{:S(2)}) async-start(f32[16,4,1,128]{3,1,2,0:T(4,128)} %copy.56), calls=%async_computation.7 | async-start | bytes 65536 | tf_op jit(solution)/shard_map/all_to_all | solution.py:61
  243.0 17.7 %all-to-all-start.8 = ((f32[1,32,256]{2,0,1:T(1,128)}), f32[1,32,256]{2,0,1:T(1,128)S(1)}, u32[]{:S(2)}, u32[]{:S(2)}) async-start(f32[1,32,256]{2,0,1:T(1,128)} %bitcast.35), calls=%async_computation.8 | async-start | bytes 65536 | tf_op jit(solution)/shard_map/all_to_all | solution.py:71
  438.5 17.5 %all-to-all-start.14 = ((f32[1,32,256]{2,0,1:T(1,128)}), f32[1,32,256]{2,0,1:T(1,128)S(1)}, u32[]{:S(2)}, u32[]{:S(2)}) async-start(f32[1,32,256]{2,0,1:T(1,128)} %bitcast.64), calls=%async_computation.14 | async-start | bytes 65536 | tf_op jit(solution)/shard_map/all_to_all | solution.py:71
  584.9 17.8 %all-to-all-start.17 = ((f32[1,32,256]{2,0,1:T(1,128)}), f32[1,32,256]{2,0,1:T(1,128)S(1)}, u32[]{:S(2)}, u32[]{:S(2)}) async-start(f32[1,32,256]{2,0,1:T(1,128)} %bitcast.84), calls=%async_computation.17 | async-start | bytes 65536 | tf_op jit(solution)/shard_map/all_to_all | solution.py:71
where the time goes:
time: 605 us; the launch traced here: 603 us
  blocking collectives  422 us (70%)
  waiting for transfers between devices  66.8 us (11%)
  other arithmetic  42.1 us (7%)
  starting transfers between devices  38.9 us (6%)
  matrix products  18.2 us (3%)
  local copies, waits for them, and re-layouts  14 us (2%)
    psum x15, blocking collectives, over_axes(): return functools.reduce(lax.psum, axes, value)  225 us
    all_to_all x5, blocking collectives, to_cases(): lax.all_to_all(values, BLK, split_axis=0, concat_axis=1, tiled=True)  108 us
    all_to_all x2, blocking collectives, copy_for_each(): return lax.all_to_all(copies, axis, split_axis=0, concat_axis=0, tiled=True)  50.9 us
    all_to_all x4, waiting for transfers between devices, to_dofs(): return lax.all_to_all(values, BLK, split_axis=1, concat_axis=0, tiled=True)  43.4 us
    all_to_all x4, blocking collectives, share(): lax.all_to_all(outgoing, SUB, split_axis=0, concat_axis=0, tiled=True)  38.5 us
    all_to_all x4, starting transfers between devices, to_dofs(): return lax.all_to_all(values, BLK, split_axis=1, concat_axis=0, tiled=True)  23 us
    all_to_all x2, waiting for transfers between devices, share(): lax.all_to_all(outgoing, SUB, split_axis=0, concat_axis=0, tiled=True)  12.1 us
  transfers between devices with their start and end apart: 7, of which 7 were waited for; matrix products, arithmetic and copies ran while one was open for 1% of the time, Pallas kernels for 0%

commit v1 on v0

v1 whole, which is shorter than its diff:
```python
import functools

import jax
import jax.numpy as jnp
from jax import lax
from jax.experimental import pallas as pl
from jax.experimental.pallas import tpu as pltpu
from jax.sharding import PartitionSpec as P

MESH = pl.DeviceIdType.MESH
HIGHEST = lax.Precision.HIGHEST
NS = 16
NB = 32
CASES = 32
ROWS = 256
NN = ((1,), (0,))
NT = ((1,), (1,))
TN = ((0,), (0,))


def mm(left, right, dims):
    return lax.dot_general(
        left, right, (dims, ((), ())), precision=HIGHEST, preferred_element_type=jnp.float32
    )


def packed(field):
    return [
        jnp.concatenate(
            [field[k * 128 + q * 32 : k * 128 + q * 32 + 32, :] for q in range(4)], axis=1
        )
        for k in range(2)
    ]


def unpacked(halves):
    return jnp.concatenate(
        [halves[k][:, q * 32 : q * 32 + 32] for k in range(2) for q in range(4)], axis=0
    )


def factor(aug):
    rows_at = lax.broadcasted_iota(jnp.int32, aug.shape, 0)
    out = jnp.zeros_like(aug)
    for step in range(CASES):
        row = aug[step : step + 1, :]
        scaled = row * lax.rsqrt(row[:, step : step + 1])
        column = aug[:, step : step + 1] * lax.rsqrt(row[:, step : step + 1])
        out = jnp.where(rows_at == step, jnp.broadcast_to(scaled, aug.shape), out)
        if step < CASES - 1:
            aug = aug - column * scaled
    return out


def kernel(
    weight_ref,
    x0_ref,
    inv_send_ref,
    inv_ref,
    slot_row_ref,
    slot_col_ref,
    schur_hbm,
    sol_ref,
    misfit_ref,
    schur,
    f1_send,
    f1_recv,
    f2_send,
    f2_recv,
    f3_send,
    f3_recv,
    n1_recv,
    n2_send,
    n2_recv,
    n3_send,
    n3_recv,
    zbuf,
    basis,
    gram_buf,
    part_buf,
    ar_core,
    ar_x,
    ar_z,
    ar_y,
    ar_out,
    schur_sem,
    send_sem,
    recv_sem,
    n_send_sem,
    n_recv_sem,
    z_send_sem,
    z_recv_sem,
    ar_send_sem,
    ar_recv_sem,
):
    sub = lax.axis_index("sub")
    blk = lax.axis_index("blk")
    x, zl = sub // 4, sub % 4
    zh, y, core = blk // 16, (blk // 2) % 8, blk % 2
    z = zh * 4 + zl
    sibling = (sub, blk + 1 - 2 * core)
    other_half = (blk + 16) % NB

    load_schur = pltpu.make_async_copy(schur_hbm, schur, schur_sem)
    load_schur.start()

    def z_peer(t):
        to = (z + t) % 8
        return (x * 4 + to % 4, (to // 4) * 16 + blk % 16)

    barrier = pltpu.get_barrier_semaphore()

    def greet(device):
        pl.semaphore_signal(barrier, inc=1, device_id=device, device_id_type=MESH)

    def greet_blk(t, _):
        greet((sub, (blk + t) % NB))
        return 0

    def greet_sub(t, _):
        greet(((sub + t) % NS, blk))
        return 0

    lax.fori_loop(1, NB, greet_blk, 0)
    lax.fori_loop(1, NS, greet_sub, 0)
    def greet_z(t, _):
        greet((x * 4 + (zl + t) % 4, other_half))
        return 0

    lax.fori_loop(1, 4, greet_z, 0)

    f2_zero = jnp.zeros((3, 1, 4, 128), jnp.float32)
    f2_recv[:, pl.ds(sub, 1)] = f2_zero
    n2_recv[pl.ds(pl.multiple_of(sub * 16, 16), 16), :] = jnp.zeros((16, 128), jnp.float32)

    slot_row = slot_row_ref[...]
    slot_col = slot_col_ref[...]
    blocks_in_lanes = lax.broadcasted_iota(jnp.int32, (64, NB), 1) * 2
    blocks_in_rows = lax.broadcasted_iota(jnp.int32, (NB, 64), 0) * 2
    pick = [(slot_col == blocks_in_lanes + k).astype(jnp.float32) for k in range(2)]
    place = [(slot_row == blocks_in_rows + k).astype(jnp.float32) for k in range(2)]
    held = [1.0 / (1.0 + jnp.sum(place[k], axis=1, keepdims=True)) for k in range(2)]

    pl.semaphore_wait(barrier, NB - 1 + NS - 1 + 3)

    def remote(src, dst, send, recv, device):
        return pltpu.make_async_remote_copy(
            src_ref=src,
            dst_ref=dst,
            send_sem=send,
            recv_sem=recv,
            device_id=device,
            device_id_type=MESH,
        )

    def wait_bytes(ref, sem):
        pltpu.make_async_copy(ref, ref, sem).wait()

    def over_blk(source, target, send, recv):
        def one(t, _):
            to = (blk + 15 + t) % NB
            remote(source(to), target(blk), send, recv, (sub, to)).start()
            return 0

        lax.fori_loop(1, NB - 15, one, 0)

        def rest(t, _):
            to = (blk + t) % NB
            remote(source(to), target(blk), send, recv, (sub, to)).start()
            return 0

        lax.fori_loop(1, 16, rest, 0)

    def over_sub(source, target, send, recv):
        def one(t, _):
            to = (sub + t) % NS
            remote(source(to), target(sub), send, recv, (to, blk)).start()
            return 0

        lax.fori_loop(1, NS, one, 0)

    def eight(ref, at):
        return ref.at[pl.ds(pl.multiple_of(at * 8, 8), 8), :]

    def sixteen(ref, at):
        return ref.at[pl.ds(pl.multiple_of(at * 16, 16), 16), :]

    def scatter_rows(r, source):
        over_blk(
            lambda to: source.at[to],
            lambda own: f1_recv.at[r, own],
            send_sem.at[r, 0],
            recv_sem.at[r, 0],
        )
        f1_recv[r, pl.ds(blk, 1)] = source[pl.ds(blk, 1)]

    def exchange(r):
        wait_bytes(f1_recv.at[r, pl.ds(0, NB - 1)], recv_sem.at[r, 0])
        own = [f1_recv[r, :, k, :] for k in range(2)]
        out = mm(pick[0], own[0], NN) + mm(pick[1], own[1], NN)
        for j in range(NS):
            f2_send[r, j] = out[4 * j : 4 * j + 4, :]
        over_sub(
            lambda to: f2_send.at[r, to],
            lambda own_sub: f2_recv.at[r, own_sub],
            send_sem.at[r, 1],
            recv_sem.at[r, 1],
        )
        return own

    def assembled(r, own):
        wait_bytes(f2_recv.at[r, pl.ds(0, NS - 1)], recv_sem.at[r, 1])
        came = jnp.concatenate([f2_recv[r, j] for j in range(NS)], axis=0)
        return [own[k] + mm(place[k], came, NN) for k in range(2)]

    def gather_rows(r, halves):
        for k in range(2):
            f3_send[r, :, k, :] = halves[k]
        over_blk(
            lambda to: f3_send.at[r, to],
            lambda own: f3_recv.at[r, own],
            send_sem.at[r, 2],
            recv_sem.at[r, 2],
        )
        f3_recv[r, pl.ds(blk, 1)] = f3_send[r, pl.ds(blk, 1)]

    def owned_rows(r):
        wait_bytes(f3_recv.at[r, pl.ds(0, NB - 1)], recv_sem.at[r, 2])
        return unpacked([f3_recv[r, :, k, :] for k in range(2)])

    def gram(r, halves):
        stacked = unpacked(halves)
        basis[:, r * 32 : r * 32 + 32] = stacked
        weighted = unpacked([halves[k] * held[k] for k in range(2)])
        return mm(weighted, basis[...], TN) * (1.0 / (NS * NB * ROWS))

    def all_reduce(r, local):
        gram_buf[r] = local
        remote(
            gram_buf.at[r, pl.ds(pl.multiple_of((1 - core) * 16, 16), 16), :],
            ar_core.at[r],
            ar_send_sem.at[r, 0],
            ar_recv_sem.at[r, 0],
            sibling,
        ).start()
        yield
        wait_bytes(ar_core.at[r], ar_recv_sem.at[r, 0])
        mine = gram_buf[r, pl.ds(pl.multiple_of(core * 16, 16), 16), :]
        came = ar_core[r]
        value = mine + came
        for phase, (buf, count, at, peer) in enumerate(
            (
                (ar_x, 4, x, lambda t: (((x + t) % 4) * 4 + zl, blk)),
                (ar_z, 8, z, z_peer),
                (ar_y, 8, y, lambda t: (sub, zh * 16 + ((y + t) % 8) * 2 + core)),
            )
        ):
            buf[r, pl.ds(at, 1)] = value[None]
            part_buf[r, phase] = value

            def one(t, _, buf=buf, at=at, peer=peer, phase=phase):
                remote(
                    part_buf.at[r, phase],
                    buf.at[r, at],
                    ar_send_sem.at[r, phase + 1],
                    ar_recv_sem.at[r, phase + 1],
                    peer(t),
                ).start()
                return 0

            lax.fori_loop(1, count, one, 0)
            yield
            wait_bytes(buf.at[r, pl.ds(0, count - 1)], ar_recv_sem.at[r, phase + 1])
            value = buf[r, 0]
            for t in range(1, count):
                value = value + buf[r, t]
        own_half = pl.ds(pl.multiple_of(core * 16, 16), 16)
        ar_out[r, own_half, :] = value
        part_buf[r, 3] = value
        remote(
            part_buf.at[r, 3],
            ar_out.at[r, own_half, :],
            ar_send_sem.at[r, 4],
            ar_recv_sem.at[r, 4],
            sibling,
        ).start()
        yield
        wait_bytes(ar_out.at[r, pl.ds(0, 16), :], ar_recv_sem.at[r, 4])
        yield

    def drain(steps):
        for _ in steps:
            pass

    def columns(r, device):
        return zbuf.at[r, :, pl.ds(pl.multiple_of(device * ROWS, ROWS), ROWS)]

    def pass_on(r, chunk, device):
        remote(
            columns(r, chunk), columns(r, chunk), z_send_sem.at[r], z_recv_sem.at[r, chunk], device
        ).start()

    def arrived(r, chunk):
        wait_bytes(columns(r, chunk), z_recv_sem.at[r, chunk])

    def along_y(r, chunk):
        def one(t, _):
            pass_on(r, chunk, (sub, zh * 16 + ((y + t) % 8) * 2 + core))
            return 0

        lax.fori_loop(1, 8, one, 0)

    def apply_schur(r, field, meanwhile):
        zbuf[r, :, pl.ds(pl.multiple_of(blk * ROWS, ROWS), ROWS)] = jnp.transpose(field).astype(
            jnp.bfloat16
        )
        pass_on(r, blk, (sub, other_half))
        along_y(r, blk)
        pass_on(r, blk, sibling)
        next(meanwhile, None)

        def to_sibling(base):
            def one(t, _):
                away = (t + 1) // 2 + (t % 2 - 1) * (2 * ((t + 1) // 2) - 8)
                chunk = base * 16 + ((y + away) % 8) * 2 + core
                arrived(r, chunk)
                pass_on(r, chunk, sibling)
                return 0

            return one

        def from_sibling(base):
            def one(t, _):
                arrived(r, base * 16 + ((y + t) % 8) * 2 + 1 - core)
                return 0

            return one

        lax.fori_loop(1, 5, to_sibling(zh), 0)
        arrived(r, other_half)
        along_y(r, other_half)
        pass_on(r, other_half, sibling)
        lax.fori_loop(5, 8, to_sibling(zh), 0)
        lax.fori_loop(0, 8, from_sibling(zh), 0)
        next(meanwhile, None)
        if r == 0:
            load_schur.wait()
        near = pl.ds(pl.multiple_of(zh * 4096, 4096), 4096)
        far = pl.ds(pl.multiple_of((1 - zh) * 4096, 4096), 4096)
        total = lax.dot_general(
            schur[:, near], zbuf[r, :, near], (NT, ((), ())), preferred_element_type=jnp.float32
        )
        next(meanwhile, None)
        lax.fori_loop(1, 8, to_sibling(1 - zh), 0)
        next(meanwhile, None)
        lax.fori_loop(0, 8, from_sibling(1 - zh), 0)
        return total + lax.dot_general(
            schur[:, far], zbuf[r, :, far], (NT, ((), ())), preferred_element_type=jnp.float32
        )

    def precondition(blocks, field):
        return jnp.concatenate(
            [mm(blocks[k], field[k * 128 : k * 128 + 128, :], NN) for k in range(2)], axis=0
        )

    identity = (
        lax.broadcasted_iota(jnp.int32, (CASES, CASES), 0)
        == lax.broadcasted_iota(jnp.int32, (CASES, CASES), 1)
    ).astype(jnp.float32)
    blank = jnp.zeros((CASES, CASES), jnp.float32)

    def with_right(matrix, *right):
        filled = (matrix, *right) + (blank,) * (3 - len(right))
        return jnp.concatenate(filled, axis=1)

    basis[...] = jnp.zeros((ROWS, 128), jnp.float32)
    scatter_rows(0, x0_ref)
    over_blk(
        lambda to: eight(inv_send_ref, to),
        lambda own: eight(n1_recv, own),
        n_send_sem.at[0],
        n_recv_sem.at[0],
    )
    n1_recv[pl.ds(pl.multiple_of(blk * 8, 8), 8), :] = inv_send_ref[
        pl.ds(pl.multiple_of(blk * 8, 8), 8), :
    ]
    own = exchange(0)
    wait_bytes(n1_recv.at[pl.ds(0, 248), :], n_recv_sem.at[0])
    for q in range(4):
        out = mm(pick[0], n1_recv[pl.ds(q, NB, stride=8), :], NN) + mm(
            pick[1], n1_recv[pl.ds(4 + q, NB, stride=8), :], NN
        )
        for j in range(NS):
            n2_send[j * 16 + q * 4 : j * 16 + q * 4 + 4, :] = out[4 * j : 4 * j + 4, :]
    over_sub(
        lambda to: sixteen(n2_send, to),
        lambda own_sub: sixteen(n2_recv, own_sub),
        n_send_sem.at[1],
        n_recv_sem.at[1],
    )
    right_side = assembled(0, own)
    gather_rows(0, right_side)
    first_sum = all_reduce(0, gram(0, right_side))
    next(first_sum)
    wait_bytes(n2_recv.at[pl.ds(0, 240), :], n_recv_sem.at[1])
    for q in range(4):
        came = jnp.concatenate(
            [n2_recv[j * 16 + q * 4 : j * 16 + q * 4 + 4, :] for j in range(NS)], axis=0
        )
        for k in range(2):
            n3_send[pl.ds(k * 4 + q, NB, stride=8), :] = mm(place[k], came, NN)
    over_blk(
        lambda to: eight(n3_send, to),
        lambda own: eight(n3_recv, own),
        n_send_sem.at[2],
        n_recv_sem.at[2],
    )
    n3_recv[pl.ds(pl.multiple_of(blk * 8, 8), 8), :] = n3_send[
        pl.ds(pl.multiple_of(blk * 8, 8), 8), :
    ]
    drain(first_sum)
    start = factor(with_right(ar_out[0][:, :32], identity))
    c0_t, c0_inv = start[:, :32], start[:, 32:64]
    v0 = mm(owned_rows(0), c0_inv, NT)
    wait_bytes(n3_recv.at[pl.ds(0, 248), :], n_recv_sem.at[2])
    blocks = [
        (
            inv_ref[k * 128 : k * 128 + 128, :]
            + jnp.concatenate(
                [n3_recv[pl.ds(k * 4 + q, NB, stride=8), :] for q in range(4)], axis=0
            )
        )
        * weight_ref[0, k]
        for k in range(2)
    ]
    mv0 = precondition(blocks, v0)

    w0 = apply_schur(0, mv0, iter(()))
    for k, half in enumerate(packed(w0)):
        f1_send[0, :, k, :] = half
    scatter_rows(1, f1_send.at[0])
    own = exchange(1)
    image = assembled(1, own)
    gather_rows(1, image)
    second_sum = all_reduce(1, gram(1, image))
    next(second_sum)
    z1 = precondition(blocks, owned_rows(1))
    next(second_sum)

    y1 = apply_schur(1, z1, second_sum)
    drain(second_sum)
    sums = ar_out[1]
    h00 = mm(sums[:, :32], c0_inv, NT)
    w0w0 = sums[:, 32:64]
    low = factor(with_right(w0w0 - mm(h00, h00, NT), identity))
    h10_t, h10_inv = low[:, :32], low[:, 32:64]
    w1 = mm(y1 - mm(w0, h00, NT), h10_inv, NT)
    for k, half in enumerate(packed(w1)):
        f1_send[1, :, k, :] = half
    scatter_rows(2, f1_send.at[1])
    h00_c0 = mm(h00, c0_t, NN)
    fact = factor(with_right(w0w0, identity, h00_c0))
    f_inv_low, f_right = fact[:, 32:64], fact[:, 64:96]
    f_inv = mm(f_inv_low, f_inv_low, TN)
    own = exchange(2)
    mv1 = mm(z1 - mm(mv0, h00, NT), h10_inv, NT)
    last = gram(2, assembled(2, own))
    drain(all_reduce(2, last))
    sums = ar_out[2]
    h01 = mm(sums[:, :32], c0_inv, NT)
    g21 = sums[:, 32:64]
    w1w1 = sums[:, 64:96]
    h11 = mm(g21 - mm(h01, h00, NT), h10_inv, NT)
    a1 = mm(f_inv_low, g21, NT)
    right = mm(h01, c0_t, NN) - mm(a1, f_right, TN)
    solved = factor(with_right(w1w1 - mm(a1, a1, TN), identity, right))
    h21_t = factor(with_right(w1w1 - mm(h01, h01, NT) - mm(h11, h11, NT)))[:, :32]
    y_1 = mm(solved[:, 64:96], solved[:, 32:64], TN)
    r0 = mm(c0_t, h00, ((0,), (1,)))
    y_0 = mm(r0 - mm(y_1, g21, NN), f_inv, NN)
    sol_ref[...] = mm(y_0, mv0, NT) + mm(y_1, mv1, NT)
    c0 = mm(c0_t, identity, TN)
    misfit_ref[:, :32] = c0 - mm(y_0, h00, NN) - mm(y_1, h01, NN)
    misfit_ref[:, 32:64] = -mm(y_0, h10_t, NT) - mm(y_1, h11, NN)
    misfit_ref[:, 64:96] = -mm(y_1, h21_t, NT)

    for r in range(3):
        wait_bytes(f1_recv.at[r, pl.ds(0, NB - 1)], send_sem.at[r, 0])
        wait_bytes(f2_recv.at[r, pl.ds(0, NS - 1)], send_sem.at[r, 1])
        if r < 2:
            wait_bytes(f3_recv.at[r, pl.ds(0, NB - 1)], send_sem.at[r, 2])
            wait_bytes(zbuf.at[r, :, pl.ds(0, 31 * ROWS)], z_send_sem.at[r])
        wait_bytes(ar_core.at[r], ar_send_sem.at[r, 0])
        wait_bytes(ar_x.at[r, pl.ds(0, 3)], ar_send_sem.at[r, 1])
        wait_bytes(ar_z.at[r, pl.ds(0, 7)], ar_send_sem.at[r, 2])
        wait_bytes(ar_y.at[r, pl.ds(0, 7)], ar_send_sem.at[r, 3])
        wait_bytes(ar_core.at[r], ar_send_sem.at[r, 4])
    wait_bytes(n1_recv.at[pl.ds(0, 248), :], n_send_sem.at[0])
    wait_bytes(n2_recv.at[pl.ds(0, 240), :], n_send_sem.at[1])
    wait_bytes(n1_recv.at[pl.ds(0, 248), :], n_send_sem.at[2])


def body(schur, inverse_blocks, loads, share_list, multiplicity):
    weight = 1.0 / multiplicity.astype(jnp.float32)
    x0 = jnp.transpose(loads[0].reshape(CASES, 2, 4, 32), (3, 1, 2, 0)).reshape(32, 2, 128)
    inverse = inverse_blocks[0]
    inv_send = jnp.transpose(inverse.reshape(2, 4, 32, 128), (2, 0, 1, 3)).reshape(256, 128)
    slots = share_list[0].reshape(1, 64)
    f32 = jnp.float32
    vmem = pl.BlockSpec(memory_space=pltpu.VMEM)
    dma = pltpu.SemaphoreType.DMA
    sol, misfit = pl.pallas_call(
        kernel,
        out_shape=(
            jax.ShapeDtypeStruct((CASES, ROWS), f32),
            jax.ShapeDtypeStruct((CASES, 96), f32),
        ),
        in_specs=[pl.BlockSpec(memory_space=pltpu.SMEM)]
        + [vmem] * 5
        + [pl.BlockSpec(memory_space=pl.ANY)],
        out_specs=(vmem, vmem),
        scratch_shapes=[
            pltpu.VMEM((256, 8192), jnp.bfloat16),
            pltpu.VMEM((2, NB, 2, 128), f32),
            pltpu.VMEM((3, NB, 2, 128), f32),
            pltpu.VMEM((3, NS, 4, 128), f32),
            pltpu.VMEM((3, NS, 4, 128), f32),
            pltpu.VMEM((2, NB, 2, 128), f32),
            pltpu.VMEM((2, NB, 2, 128), f32),
            pltpu.VMEM((256, 128), f32),
            pltpu.VMEM((256, 128), f32),
            pltpu.VMEM((256, 128), f32),
            pltpu.VMEM((256, 128), f32),
            pltpu.VMEM((256, 128), f32),
            pltpu.VMEM((2, CASES, 8192), jnp.bfloat16),
            pltpu.VMEM((256, 128), f32),
            pltpu.VMEM((3, 32, 128), f32),
            pltpu.VMEM((3, 4, 16, 128), f32),
            pltpu.VMEM((3, 16, 128), f32),
            pltpu.VMEM((3, 4, 16, 128), f32),
            pltpu.VMEM((3, 8, 16, 128), f32),
            pltpu.VMEM((3, 8, 16, 128), f32),
            pltpu.VMEM((3, 32, 128), f32),
            dma,
            dma((3, 3)),
            dma((3, 3)),
            dma((3,)),
            dma((3,)),
            dma((2,)),
            dma((2, NB)),
            dma((3, 5)),
            dma((3, 5)),
        ],
        compiler_params=pltpu.CompilerParams(collective_id=0, has_side_effects=True),
    )(
        weight,
        x0,
        inv_send,
        inverse.reshape(256, 128),
        slots,
        slots.reshape(64, 1),
        schur[0],
    )
    return sol[None], misfit


def solution(mesh):
    placed = (
        P("sub", "blk", None),
        P("sub", "blk", None, None),
        P("sub", None, "blk"),
        P("sub", None, None),
        P("sub", "blk"),
    )
    return jax.shard_map(
        body, mesh=mesh, in_specs=placed, out_specs=(P("sub", None, "blk"), P()), check_vma=False
    )
```

time: 605 us -> 148 us (0.24)
  blocking collectives: 422 us -> 0 us
  Pallas kernels: 0 us -> 138 us
  waiting for transfers between devices: 66.8 us -> 0 us
  other arithmetic: 42.1 us -> 1.17 us
  starting transfers between devices: 38.9 us -> 0 us
  matrix products: 18.2 us -> 0 us
    psum x15 -> x0, blocking collectives: 225 us -> none  [over_axes(): return functools.reduce(lax.psum, axes, value)]
    all_to_all x11 -> x0, blocking collectives: 197 us -> none  [the longest x5 108 us: to_cases(): lax.all_to_all(values, BLK, split_axis=0, concat_axis=1, tiled=True)]
    pallas_call x0 -> x1, Pallas kernels: none -> 138 us  [body(): pl.pallas_call(kernel, out_shape=(jax.ShapeDtypeStruct((CASES, ROWS), f32...]
    all_to_all x7 -> x0, waiting for transfers between devices: 66.8 us -> none  [the longest x4 43.4 us: to_dofs(): return lax.all_to_all(values, BLK, split_axis=1, concat_axis=0, tiled=True)]
    all_to_all x7 -> x0, starting transfers between devices: 38.9 us -> none  [the longest x4 23 us: to_dofs(): return lax.all_to_all(values, BLK, split_axis=1, concat_axis=0, tiled=True)]
    another operation x21 -> x0, other arithmetic: 33.1 us -> none  [the longest x3 7.48 us: lower_solve(): return jax.scipy.linalg.solve_triangular(lower, values, lower=True)]
    dot_general x30 -> x0, matrix products: 17.4 us -> none  [the longest x2 6.82 us: body(): lax.dot_general(gathered_copies(rounded, BLK, 0), matrix, (((1,), (1,)),...]
    broadcast_in_dim x2 -> x0, other arithmetic: 7.62 us -> none  [copy_for_each(): copies = jnp.broadcast_to(value, (lax.axis_size(axis), *value.shape))]
  transfers between devices with their start and end apart: 7 -> 0, of which waited for: 7 -> 0; matrix products, arithmetic and copies ran while one was open for 1% -> 0% of each run, Pallas kernels for 0% -> 0%
where the time goes in v1:
time: 148 us
  Pallas kernels  138 us (93%)
  local copies, waits for them, and re-layouts  8.12 us (5%)
    pallas_call x1, Pallas kernels, body(): pl.pallas_call(kernel, out_shape=(jax.ShapeDtypeStruct((CASES, ROWS), f32...  138 us
    unnamed x3, local copies, waits for them, and re-layouts  3.46 us

profile of v1, /device:TPU:1, one launch (start us, length us, event | category | flops | bytes accessed | tf_op | source)
XLA Modules:
  0.0 147.5 jit_solution(5092260238164615199)
XLA Ops:
  0.6 1.2 convert_divide_fusion.weight_ref
  1.8 0.9 reshape_squeeze.12
  2.7 0.1 copy.12
  2.8 0.8 reshape.10.x0_ref
  3.6 1.6 %copy.13 = f32[2,4,32,128]{3,1,0,2:T(4,128)} copy(f32[2,4,32,128]{3,2,1,0:T(8,128)} %bitcast.9) | data formatting | bytes 262144 | tf_op jit(solution)/shard_map/reshape;squeeze | solution.py:507
  5.2 0.8 copy.14
  6.0 0.6 reshape_squeeze.15.slot_row_ref
  6.6 0.7 reshape_reshape_squeeze.4.slot_col_ref
  7.2 137.6 %shard_map.68 = (f32[32,256]{1,0:T(8,128)}, f32[32,96]{1,0:T(8,128)}) custom-call(f32[1,2]{1,0:T(1,128)} %convert_divide_fusion.weight_ref, f32[32,2,128]{2,1,0:T(2,128)} %reshape.10.x0_ref, f32[256,128]{1,0:T(8,128)} %bitcast.11, f32[256,128]{1,0:T(8,128)} %bitcast.10, s32[1,64]{1,0:T(1,128)} %reshape_squeeze.15.slot_row_ref, ...), custom_call_target="tpu_custom_call" | custom-call | tf_op jit(solution)/shard_map/pallas_call | solution.py:512
  144.8 1.4 copy.19
  146.2 1.3 copy.20

commit v2 on v1

v2 whole, which is shorter than its diff:
```python
import functools

import jax
import jax.numpy as jnp
from jax import lax
from jax.experimental import pallas as pl
from jax.experimental.pallas import tpu as pltpu
from jax.sharding import PartitionSpec as P

MESH = pl.DeviceIdType.MESH
HIGHEST = lax.Precision.HIGHEST
NS = 16
NB = 32
CASES = 32
ROWS = 256
NN = ((1,), (0,))
NT = ((1,), (1,))
TN = ((0,), (0,))


def mm(left, right, dims):
    return lax.dot_general(
        left, right, (dims, ((), ())), precision=HIGHEST, preferred_element_type=jnp.float32
    )


def packed(field):
    return [
        jnp.concatenate(
            [field[k * 128 + q * 32 : k * 128 + q * 32 + 32, :] for q in range(4)], axis=1
        )
        for k in range(2)
    ]


def unpacked(halves):
    return jnp.concatenate(
        [halves[k][:, q * 32 : q * 32 + 32] for k in range(2) for q in range(4)], axis=0
    )


def factor(*augs):
    augs = list(augs)
    done = [[] for _ in augs]
    lanes = (1, 128)
    for first in range(0, CASES, 4):
        for which, aug in enumerate(augs):
            rows = [aug[first + i : first + i + 1, :] for i in range(4)]
            spot = {
                (i, k): jnp.broadcast_to(rows[i][:, first + k : first + k + 1], lanes)
                for i in range(4)
                for k in range(i + 1)
            }
            columns = [
                jnp.broadcast_to(aug[:, first + i : first + i + 1], aug.shape) for i in range(4)
            ]
            low, scale = {}, []
            for i in range(4):
                for k in range(i):
                    value = spot[i, k]
                    for m in range(k):
                        value = value - low[i, m] * low[k, m]
                    low[i, k] = value * scale[k]
                value = spot[i, i]
                for m in range(i):
                    value = value - low[i, m] * low[i, m]
                scale.append(lax.rsqrt(value))
            for i in range(4):
                for m in range(i):
                    rows[i] = rows[i] - low[i, m] * rows[m]
                    columns[i] = columns[i] - low[i, m] * columns[m]
                rows[i] = rows[i] * scale[i]
                columns[i] = columns[i] * scale[i]
            done[which] += rows
            if first + 4 < CASES:
                for i in range(4):
                    aug = aug - columns[i] * rows[i]
                augs[which] = aug
    return [jnp.concatenate(rows, axis=0) for rows in done]


def folded(grams):
    return jnp.concatenate(
        [
            jnp.concatenate([gram[8 * i : 8 * i + 8, :] for i in range(4)], axis=1)
            for gram in grams
        ],
        axis=0,
    )


def unfolded(rows):
    return [
        jnp.concatenate([rows[8 * g : 8 * g + 8, 32 * i : 32 * i + 32] for i in range(4)], axis=0)
        for g in range(rows.shape[0] // 8)
    ]


def kernel(
    multiplicity_ref,
    share_ref,
    loads_hbm,
    inv_hbm,
    schur_hbm,
    sol_ref,
    misfit_ref,
    schur,
    f1_send,
    f1_recv,
    f2_send,
    f2_recv,
    f3_send,
    f3_recv,
    n1_send,
    n1_recv,
    n2_send,
    n2_recv,
    n3_send,
    n3_recv,
    zbuf,
    product,
    loads_buf,
    inv_buf,
    part_buf,
    ar_x,
    ar_z,
    ar_y,
    ar_core,
    schur_sem,
    input_sem,
    send_sem,
    recv_sem,
    n_send_sem,
    n_recv_sem,
    z_send_sem,
    z_recv_sem,
    ar_send_sem,
    ar_recv_sem,
):
    sub = lax.axis_index("sub")
    blk = lax.axis_index("blk")
    x, zl = sub // 4, sub % 4
    zh, y, core = blk // 16, (blk // 2) % 8, blk % 2
    z = zh * 4 + zl
    sibling = (sub, blk + 1 - 2 * core)
    other_half = (blk + 16) % NB

    load_loads = pltpu.make_async_copy(loads_hbm, loads_buf, input_sem.at[0])
    load_loads.start()
    load_inv = pltpu.make_async_copy(inv_hbm, inv_buf, input_sem.at[1])
    load_inv.start()

    def z_peer(t):
        to = (z + t) % 8
        return (x * 4 + to % 4, (to // 4) * 16 + blk % 16)

    barrier = pltpu.get_barrier_semaphore()

    def greet(device):
        pl.semaphore_signal(barrier, inc=1, device_id=device, device_id_type=MESH)

    def greet_blk(t, _):
        greet((sub, (blk + 15 + t) % NB))
        return 0

    def greet_near(t, _):
        greet((sub, (blk + t) % NB))
        return 0

    def greet_sub(t, _):
        greet(((sub + t) % NS, blk))
        return 0

    def greet_z(t, _):
        greet((x * 4 + (zl + t) % 4, other_half))
        return 0

    lax.fori_loop(1, NB - 15, greet_blk, 0)
    lax.fori_loop(1, 4, greet_z, 0)
    lax.fori_loop(1, 16, greet_near, 0)
    lax.fori_loop(1, NS, greet_sub, 0)

    def load_columns(chunk, _):
        at = (chunk // 16) * 16 + (chunk % 2) * 8 + (chunk // 2) % 8
        pltpu.make_async_copy(
            schur_hbm.at[:, pl.ds(pl.multiple_of(chunk * ROWS, ROWS), ROWS)],
            schur.at[:, pl.ds(pl.multiple_of(at * ROWS, ROWS), ROWS)],
            schur_sem,
        ).start()
        return 0

    lax.fori_loop(0, NB, load_columns, 0)

    f2_zero = jnp.zeros((3, 1, 4, 128), jnp.float32)
    f2_recv[:, pl.ds(sub, 1)] = f2_zero
    n2_recv[pl.ds(pl.multiple_of(sub * 16, 16), 16), :] = jnp.zeros((16, 128), jnp.float32)

    slot_at = lax.broadcasted_iota(jnp.int32, (NB, 64), 1)
    slots = jnp.full((NB, 64), -1, jnp.int32)
    for m in range(64):
        slots = jnp.where(slot_at == m, share_ref[0, m // 4, m % 4], slots)
    block_at = lax.broadcasted_iota(jnp.int32, (NB, 64), 0) * 2
    place = [(slots == block_at + k).astype(jnp.float32) for k in range(2)]
    pick = [jnp.transpose(place[k]) for k in range(2)]
    held = [1.0 / (1.0 + jnp.sum(place[k], axis=1, keepdims=True)) for k in range(2)]

    load_loads.wait()
    for k, half in enumerate(packed(jnp.transpose(loads_buf[0]))):
        f1_send[0, :, k, :] = half
    load_inv.wait()
    for k in range(2):
        for q in range(4):
            n1_send[pl.ds(k * 4 + q, NB, stride=8), :] = inv_buf[0, k, q * 32 : q * 32 + 32, :]

    pl.semaphore_wait(barrier, NB - 1 + NS - 1 + 3)

    def remote(src, dst, send, recv, device):
        return pltpu.make_async_remote_copy(
            src_ref=src,
            dst_ref=dst,
            send_sem=send,
            recv_sem=recv,
            device_id=device,
            device_id_type=MESH,
        )

    def wait_bytes(ref, sem):
        pltpu.make_async_copy(ref, ref, sem).wait()

    def over_blk(source, target, send, recv):
        def one(t, _):
            to = (blk + 15 + t) % NB
            remote(source(to), target(blk), send, recv, (sub, to)).start()
            return 0

        lax.fori_loop(1, NB - 15, one, 0)

        def rest(t, _):
            to = (blk + t) % NB
            remote(source(to), target(blk), send, recv, (sub, to)).start()
            return 0

        lax.fori_loop(1, 16, rest, 0)

    def over_sub(source, target, send, recv):
        def one(t, _):
            to = (sub + t) % NS
            remote(source(to), target(sub), send, recv, (to, blk)).start()
            return 0

        lax.fori_loop(1, NS, one, 0)

    def eight(ref, at):
        return ref.at[pl.ds(pl.multiple_of(at * 8, 8), 8), :]

    def sixteen(ref, at):
        return ref.at[pl.ds(pl.multiple_of(at * 16, 16), 16), :]

    def scatter_rows(r, source):
        over_blk(
            lambda to: source.at[to],
            lambda own: f1_recv.at[r, own],
            send_sem.at[r, 0],
            recv_sem.at[r, 0],
        )
        f1_recv[r, pl.ds(blk, 1)] = source[pl.ds(blk, 1)]

    def exchange(r):
        wait_bytes(f1_recv.at[r, pl.ds(0, NB - 1)], recv_sem.at[r, 0])
        own = [f1_recv[r, :, k, :] for k in range(2)]
        out = mm(pick[0], own[0], NN) + mm(pick[1], own[1], NN)
        for j in range(NS):
            f2_send[r, j] = out[4 * j : 4 * j + 4, :]
        over_sub(
            lambda to: f2_send.at[r, to],
            lambda own_sub: f2_recv.at[r, own_sub],
            send_sem.at[r, 1],
            recv_sem.at[r, 1],
        )
        return own

    def assembled(r, own):
        wait_bytes(f2_recv.at[r, pl.ds(0, NS - 1)], recv_sem.at[r, 1])
        came = jnp.concatenate([f2_recv[r, j] for j in range(NS)], axis=0)
        return [own[k] + mm(place[k], came, NN) for k in range(2)]

    def gather_rows(r, halves):
        for k in range(2):
            f3_send[r, :, k, :] = halves[k]
        over_blk(
            lambda to: f3_send.at[r, to],
            lambda own: f3_recv.at[r, own],
            send_sem.at[r, 2],
            recv_sem.at[r, 2],
        )
        f3_recv[r, pl.ds(blk, 1)] = f3_send[r, pl.ds(blk, 1)]

    def owned_rows(r):
        wait_bytes(f3_recv.at[r, pl.ds(0, NB - 1)], recv_sem.at[r, 2])
        return unpacked([f3_recv[r, :, k, :] for k in range(2)])

    def stacked(halves):
        weighted = unpacked([halves[k] * held[k] for k in range(2)])
        return weighted, unpacked(halves)

    def grams(left, *rights):
        scale = 1.0 / (NS * NB * ROWS)
        return folded([mm(left, right, TN) * scale for right in rights])

    def all_reduce(r, value):
        rows = value.shape[0]
        used = pl.ds(0, rows)
        for phase, (buf, count, at, peer) in enumerate(
            (
                (ar_x, 4, x, lambda t: (((x + t) % 4) * 4 + zl, blk)),
                (ar_z, 8, z, z_peer),
                (ar_y, 8, y, lambda t: (sub, zh * 16 + ((y + t) % 8) * 2 + core)),
                (ar_core, 2, core, lambda t: sibling),
            )
        ):
            part_buf[r, phase, :rows] = value
            buf[r, pl.ds(at, 1), :rows] = value[None]

            def one(t, _, buf=buf, at=at, peer=peer, phase=phase):
                remote(
                    part_buf.at[r, phase, used],
                    buf.at[r, at, used],
                    ar_send_sem.at[r, phase],
                    ar_recv_sem.at[r, phase],
                    peer(t),
                ).start()
                return 0

            lax.fori_loop(1, count, one, 0)
            yield None
            wait_bytes(buf.at[r, pl.ds(0, count - 1), used], ar_recv_sem.at[r, phase])
            value = buf[r, 0, :rows]
            for t in range(1, count):
                value = value + buf[r, t, :rows]
        result = unfolded(value)
        while True:
            yield result

    def drain(steps):
        while (result := next(steps)) is None:
            pass
        return result

    def columns(r, at):
        return zbuf.at[r, :, pl.ds(pl.multiple_of(at * ROWS, ROWS), ROWS)]

    def pass_on(r, at, device):
        remote(
            columns(r, at), columns(r, at), z_send_sem.at[r], z_recv_sem.at[r, at], device
        ).start()

    def arrived(r, at):
        wait_bytes(columns(r, at), z_recv_sem.at[r, at])

    def along_y(r, at):
        def one(t, _):
            pass_on(r, at, (sub, zh * 16 + ((y + t) % 8) * 2 + core))
            return 0

        lax.fori_loop(1, 8, one, 0)

    def apply_schur(r, field, meanwhile):
        mine = zh * 16 + core * 8
        far_mine = (1 - zh) * 16 + core * 8
        zbuf[r, :, pl.ds(pl.multiple_of((mine + y) * ROWS, ROWS), ROWS)] = jnp.transpose(
            field
        ).astype(jnp.bfloat16)
        pass_on(r, mine + y, (sub, other_half))
        along_y(r, mine + y)
        pass_on(r, mine + y, sibling)
        next(meanwhile, None)

        def to_sibling(base):
            def one(t, _):
                away = (t + 1) // 2 + (t % 2 - 1) * (2 * ((t + 1) // 2) - 8)
                at = base + (y + away) % 8
                arrived(r, at)
                pass_on(r, at, sibling)
                return 0

            return one

        def from_sibling(base):
            def one(t, _):
                arrived(r, base + (y + t) % 8)
                return 0

            return one

        def multiply(base, fresh=False):
            part = pl.ds(pl.multiple_of(base * ROWS, 2048), 2048)
            term = lax.dot_general(
                schur[:, part], zbuf[r, :, part], (NT, ((), ())), preferred_element_type=jnp.float32
            )
            return term if fresh else product[...] + term

        lax.fori_loop(1, 5, to_sibling(mine), 0)
        arrived(r, far_mine + y)
        along_y(r, far_mine + y)
        pass_on(r, far_mine + y, sibling)
        lax.fori_loop(5, 8, to_sibling(mine), 0)
        if r == 0:
            wait_bytes(schur, schur_sem)
        product[...] = multiply(mine, True)
        next(meanwhile, None)
        lax.fori_loop(0, 8, from_sibling(zh * 16 + (1 - core) * 8), 0)
        product[...] = multiply(zh * 16 + (1 - core) * 8)
        next(meanwhile, None)
        lax.fori_loop(1, 8, to_sibling(far_mine), 0)
        product[...] = multiply(far_mine)
        next(meanwhile, None)
        lax.fori_loop(0, 8, from_sibling((1 - zh) * 16 + (1 - core) * 8), 0)
        return multiply((1 - zh) * 16 + (1 - core) * 8)

    def precondition(blocks, field):
        return jnp.concatenate(
            [mm(blocks[k], field[k * 128 : k * 128 + 128, :], NN) for k in range(2)], axis=0
        )

    identity = (
        lax.broadcasted_iota(jnp.int32, (CASES, CASES), 0)
        == lax.broadcasted_iota(jnp.int32, (CASES, CASES), 1)
    ).astype(jnp.float32)
    blank = jnp.zeros((CASES, CASES), jnp.float32)

    def with_right(matrix, *right):
        filled = (matrix, *right) + (blank,) * (3 - len(right))
        return jnp.concatenate(filled, axis=1)

    scatter_rows(0, f1_send.at[0])
    over_blk(
        lambda to: eight(n1_send, to),
        lambda own: eight(n1_recv, own),
        n_send_sem.at[0],
        n_recv_sem.at[0],
    )
    n1_recv[pl.ds(pl.multiple_of(blk * 8, 8), 8), :] = n1_send[
        pl.ds(pl.multiple_of(blk * 8, 8), 8), :
    ]
    own = exchange(0)
    wait_bytes(n1_recv.at[pl.ds(0, 248), :], n_recv_sem.at[0])
    for q in range(4):
        out = mm(pick[0], n1_recv[pl.ds(q, NB, stride=8), :], NN) + mm(
            pick[1], n1_recv[pl.ds(4 + q, NB, stride=8), :], NN
        )
        for j in range(NS):
            n2_send[j * 16 + q * 4 : j * 16 + q * 4 + 4, :] = out[4 * j : 4 * j + 4, :]
    over_sub(
        lambda to: sixteen(n2_send, to),
        lambda own_sub: sixteen(n2_recv, own_sub),
        n_send_sem.at[1],
        n_recv_sem.at[1],
    )
    right_side = assembled(0, own)
    gather_rows(0, right_side)
    first_sum = all_reduce(0, grams(*stacked(right_side)))
    next(first_sum)
    wait_bytes(n2_recv.at[pl.ds(0, 240), :], n_recv_sem.at[1])
    for q in range(4):
        came = jnp.concatenate(
            [n2_recv[j * 16 + q * 4 : j * 16 + q * 4 + 4, :] for j in range(NS)], axis=0
        )
        for k in range(2):
            n3_send[pl.ds(k * 4 + q, NB, stride=8), :] = mm(place[k], came, NN)
    over_blk(
        lambda to: eight(n3_send, to),
        lambda own: eight(n3_recv, own),
        n_send_sem.at[2],
        n_recv_sem.at[2],
    )
    n3_recv[pl.ds(pl.multiple_of(blk * 8, 8), 8), :] = n3_send[
        pl.ds(pl.multiple_of(blk * 8, 8), 8), :
    ]
    (b_gram,) = drain(first_sum)
    (start,) = factor(with_right(b_gram, identity))
    c0_t, c0_inv = start[:, :32], start[:, 32:64]
    b_rows = owned_rows(0)
    v0 = mm(b_rows, c0_inv, NT)
    wait_bytes(n3_recv.at[pl.ds(0, 248), :], n_recv_sem.at[2])
    blocks = [
        (
            inv_buf[0, k]
            + jnp.concatenate(
                [n3_recv[pl.ds(k * 4 + q, NB, stride=8), :] for q in range(4)], axis=0
            )
        )
        * (1.0 / jnp.full((1, 128), multiplicity_ref[0, k].astype(jnp.float32)))
        for k in range(2)
    ]
    mv0 = precondition(blocks, v0)

    w0 = apply_schur(0, mv0, iter(()))
    for k, half in enumerate(packed(w0)):
        f1_send[1, :, k, :] = half
    scatter_rows(1, f1_send.at[1])
    own = exchange(1)
    image = assembled(1, own)
    gather_rows(1, image)
    weighted, plain = stacked(image)
    second_sum = all_reduce(1, grams(weighted, stacked(right_side)[1], plain))
    next(second_sum)
    w0_rows = owned_rows(1)
    z1 = precondition(blocks, w0_rows)
    next(second_sum)

    y1 = apply_schur(1, z1, second_sum)
    w0b, w0w0 = drain(second_sum)
    h00 = mm(w0b, c0_inv, NT)
    (low,) = factor(with_right(w0w0 - mm(h00, h00, NT), identity))
    h10_t, h10_inv = low[:, :32], low[:, 32:64]
    w1 = mm(y1 - mm(w0, h00, NT), h10_inv, NT)
    for k, half in enumerate(packed(w1)):
        f1_send[2, :, k, :] = half
    scatter_rows(2, f1_send.at[2])
    third_sum = all_reduce(2, grams(w1, b_rows, w0_rows))
    next(third_sum)
    h00_c0 = mm(h00, c0_t, NN)
    (fact,) = factor(with_right(w0w0, identity, h00_c0))
    f_inv_low, f_right = fact[:, 32:64], fact[:, 64:96]
    f_inv = mm(f_inv_low, f_inv_low, TN)
    own = exchange(2)
    next(third_sum)
    mv1 = mm(z1 - mm(mv0, h00, NT), h10_inv, NT)
    c0 = mm(c0_t, identity, TN)
    r0_f = mm(mm(c0_t, h00, ((0,), (1,))), f_inv, NN)
    sol_base = mm(r0_f, mv0, NT)
    misfit_base = (c0 - mm(r0_f, h00, NN), -mm(r0_f, h10_t, NT))
    last_sum = all_reduce(3, grams(*stacked(assembled(2, own))))
    next(last_sum)
    next(third_sum)
    next(last_sum)
    next(third_sum)
    next(last_sum)
    w1b, w1w0 = drain(third_sum)
    h01 = mm(w1b, c0_inv, NT)
    h11 = mm(w1w0 - mm(h01, h00, NT), h10_inv, NT)
    a1 = mm(f_inv_low, w1w0, NT)
    right = mm(h01, c0_t, NN) - mm(a1, f_right, TN)
    w1w0_f = mm(w1w0, f_inv, NN)
    a1a1 = mm(a1, a1, TN)
    hh = mm(h01, h01, NT) + mm(h11, h11, NT)
    sol_step = mv1 - mm(mv0, w1w0_f, NT)
    misfit_step = (h01 - mm(w1w0_f, h00, NN), h11 - mm(w1w0_f, h10_t, NT))
    (w1w1,) = drain(last_sum)
    solved, last = factor(with_right(w1w1 - a1a1, identity, right), with_right(w1w1 - hh))
    y_1 = mm(solved[:, 64:96], solved[:, 32:64], TN)
    sol_ref[...] = sol_base + mm(y_1, sol_step, NT)
    misfit_ref[:, :32] = misfit_base[0] - mm(y_1, misfit_step[0], NN)
    misfit_ref[:, 32:64] = misfit_base[1] - mm(y_1, misfit_step[1], NN)
    misfit_ref[:, 64:96] = -mm(y_1, last[:, :32], NT)

    for r in range(3):
        wait_bytes(f1_recv.at[r, pl.ds(0, NB - 1)], send_sem.at[r, 0])
        wait_bytes(f2_recv.at[r, pl.ds(0, NS - 1)], send_sem.at[r, 1])
        if r < 2:
            wait_bytes(f3_recv.at[r, pl.ds(0, NB - 1)], send_sem.at[r, 2])
            wait_bytes(zbuf.at[r, :, pl.ds(0, 31 * ROWS)], z_send_sem.at[r])
    for r, rows in enumerate((8, 16, 16, 8)):
        used = pl.ds(0, rows)
        wait_bytes(ar_x.at[r, pl.ds(0, 3), used], ar_send_sem.at[r, 0])
        wait_bytes(ar_z.at[r, pl.ds(0, 7), used], ar_send_sem.at[r, 1])
        wait_bytes(ar_y.at[r, pl.ds(0, 7), used], ar_send_sem.at[r, 2])
        wait_bytes(ar_core.at[r, pl.ds(0, 1), used], ar_send_sem.at[r, 3])
    wait_bytes(n1_recv.at[pl.ds(0, 248), :], n_send_sem.at[0])
    wait_bytes(n2_recv.at[pl.ds(0, 240), :], n_send_sem.at[1])
    wait_bytes(n1_recv.at[pl.ds(0, 248), :], n_send_sem.at[2])


def body(schur, inverse_blocks, loads, share_list, multiplicity):
    f32 = jnp.float32
    vmem = pl.BlockSpec(memory_space=pltpu.VMEM)
    dma = pltpu.SemaphoreType.DMA
    sol, misfit = pl.pallas_call(
        kernel,
        out_shape=(
            jax.ShapeDtypeStruct((CASES, ROWS), f32),
            jax.ShapeDtypeStruct((CASES, 96), f32),
        ),
        in_specs=[pl.BlockSpec(memory_space=pltpu.SMEM)] * 2
        + [pl.BlockSpec(memory_space=pl.ANY)] * 3,
        out_specs=(vmem, vmem),
        scratch_shapes=[
            pltpu.VMEM((256, 8192), jnp.bfloat16),
            pltpu.VMEM((3, NB, 2, 128), f32),
            pltpu.VMEM((3, NB, 2, 128), f32),
            pltpu.VMEM((3, NS, 4, 128), f32),
            pltpu.VMEM((3, NS, 4, 128), f32),
            pltpu.VMEM((2, NB, 2, 128), f32),
            pltpu.VMEM((2, NB, 2, 128), f32),
            pltpu.VMEM((256, 128), f32),
            pltpu.VMEM((256, 128), f32),
            pltpu.VMEM((256, 128), f32),
            pltpu.VMEM((256, 128), f32),
            pltpu.VMEM((256, 128), f32),
            pltpu.VMEM((256, 128), f32),
            pltpu.VMEM((2, CASES, 8192), jnp.bfloat16),
            pltpu.VMEM((ROWS, CASES), f32),
            pltpu.VMEM((1, CASES, ROWS), f32),
            pltpu.VMEM((1, 2, 128, 128), f32),
            pltpu.VMEM((4, 4, 16, 128), f32),
            pltpu.VMEM((4, 4, 16, 128), f32),
            pltpu.VMEM((4, 8, 16, 128), f32),
            pltpu.VMEM((4, 8, 16, 128), f32),
            pltpu.VMEM((4, 2, 16, 128), f32),
            dma,
            dma((2,)),
            dma((3, 3)),
            dma((3, 3)),
            dma((3,)),
            dma((3,)),
            dma((2,)),
            dma((2, NB)),
            dma((4, 4)),
            dma((4, 4)),
        ],
        compiler_params=pltpu.CompilerParams(collective_id=0, has_side_effects=True),
    )(multiplicity, share_list, loads, inverse_blocks, schur[0])
    return sol[None], misfit


def solution(mesh):
    placed = (
        P("sub", "blk", None),
        P("sub", "blk", None, None),
        P("sub", None, "blk"),
        P("sub", None, None),
        P("sub", "blk"),
    )
    return jax.shard_map(
        body, mesh=mesh, in_specs=placed, out_specs=(P("sub", None, "blk"), P()), check_vma=False
    )
```

time: 148 us -> 132 us (0.89)
  Pallas kernels: 138 us -> 127 us
  local copies, waits for them, and re-layouts: 8.12 us -> 4.05 us
    pallas_call x1, Pallas kernels: 138 us -> 127 us  [body(): pl.pallas_call(kernel, out_shape=(jax.ShapeDtypeStruct((CASES, ROWS), f32...]
    another operation x5 -> x0, local copies, waits for them, and re-layouts: 3.92 us -> none  [the longest x1 1.64 us: body(): inverse.reshape(2, 4, 32, 128)]
where the time goes in v2:
time: 132 us
  Pallas kernels  127 us (96%)
  local copies, waits for them, and re-layouts  4.05 us (3%)
    pallas_call x1, Pallas kernels, body(): pl.pallas_call(kernel, out_shape=(jax.ShapeDtypeStruct((CASES, ROWS), f32...  127 us
    unnamed x3, local copies, waits for them, and re-layouts  4.05 us

profile of v2, /device:TPU:1, one launch (start us, length us, event | category | flops | bytes accessed | tf_op | source)
XLA Modules:
  0.0 131.5 jit_solution(9808706079342550167)
XLA Ops:
  0.6 1.4 %copy.7.share_ref = s32[1,16,4]{2,1,0:T(8,128)} copy(s32[1,16,4]{1,2,0:T(4,128)} %param.8) | data formatting | bytes 512 | tf_op args[3]
  2.0 126.8 %shard_map.68 = (f32[32,256]{1,0:T(8,128)}, f32[32,96]{1,0:T(8,128)}) custom-call(s32[1,2]{1,0:T(1,128)} %multiplicity_ref.1, s32[1,16,4]{2,1,0:T(8,128)} %copy.7.share_ref, f32[1,32,256]{2,1,0:T(8,128)} %loads_hbm.1, f32[1,2,128,128]{3,2,1,0:T(8,128)} %inv_hbm.1, bf16[256,8192]{1,0:T(8,128)(2,1)} %bitcast.2), custom_call_target="tpu_custom_call" | custom-call | tf_op jit(solution)/shard_map/pallas_call | solution.py:578
  128.8 1.4 %copy.10 = f32[1,32,256]{2,1,0:T(8,128)} copy(f32[1,32,256]{2,1,0:T(8,128)} %bitcast.3) | data formatting | bytes 65536
  130.2 1.3 %copy.11 = f32[32,96]{1,0:T(8,128)} copy(f32[32,96]{1,0:T(8,128)} %get-tuple-element.9) | data formatting | bytes 24576
